TPU v7x, 32 devices: a whole 2x2x4 slice. The times are simulated.
32 devices in a mesh: prow: 4 (over y, x), pcol: 8 (over z, core).
Axes of the slice: x: 2, y: 2, z: 4, core: 2. Of those that a mesh axis runs over, the one named last changes fastest.
Arguments:
- matrix: float32 [16, 4, 256, 8, 8, 256], P(None, 'prow', None, None, 'pcol'), may hold values from -6 to 6, as said below
- factor: float32 [16, 4, 256, 8, 8, 256], P(None, 'prow', None, None, 'pcol'), may hold values from -3 to 3, as said below
Outputs:
- reduced: float32 [16, 4, 256, 8, 8, 256], P(None, 'prow', None, None, 'pcol')
Inputs may be any that keep to these rules, and one draw needn't show every extreme that they name: Symmetric matrix stored in its lower triangle: every entry above the diagonal is zero. `factor`: lower triangular with diagonal entries between 1 and 3; every entry above the diagonal is zero.
All inputs are finite; a program needn't handle non-finite values.
Results may differ from a plain program's by a relative error of at most 0.0001.
Values sent between devices are 32-bit elements; how exact they have to be, the bound alone decides.
A program may use at most 256 MiB of HBM per device.

v0:
```python
import jax
import jax.numpy as jnp
from jax import lax
from jax.sharding import PartitionSpec as P

BLOCKS = 2
highest = lax.Precision.HIGHEST


def spread(block, axis, source):
    block = jnp.where(lax.axis_index(axis) == source, block, jnp.zeros_like(block))
    return lax.psum(block, axis)


def product(left, right):
    return jnp.dot(left, right, precision=highest, preferred_element_type=jnp.float32)


def product_trans(left, right):
    return lax.dot_general(
        left, right, (((1,), (1,)), ((), ())), precision=highest, preferred_element_type=jnp.float32
    )


def diagonal_core(diag_block, diag_factor, width):
    identity = jnp.eye(width, dtype=jnp.float32)
    inverse = lax.linalg.triangular_solve(diag_factor, identity, left_side=True, lower=True)
    symmetric = diag_block + diag_block.T - jnp.diag(jnp.diagonal(diag_block))
    inner = product_trans(product(inverse, symmetric), inverse)
    return (inverse, 0.5 * (inner + inner.T))


def on_device(matrix, factor):
    row_tiles = matrix.shape[0]
    width = matrix.shape[2]
    col_tiles = matrix.shape[3]
    prow_count = lax.axis_size("prow")
    pcol_count = lax.axis_size("pcol")
    prow_index = lax.axis_index("prow")
    pcol_index = lax.axis_index("pcol")
    height = row_tiles * width
    local = matrix.reshape(height, col_tiles * width)
    factor_local = factor.reshape(height, col_tiles * width)
    tile_rows = jnp.arange(row_tiles, dtype=jnp.int32) * prow_count + prow_index
    tile_cols = jnp.arange(col_tiles, dtype=jnp.int32) * pcol_count + pcol_index
    offsets = jnp.arange(width, dtype=jnp.int32)
    elem_rows = (tile_rows[:, None] * width + offsets[None, :]).reshape(height)
    elem_cols = (tile_cols[:, None] * width + offsets[None, :]).reshape(col_tiles * width)
    lower_part = elem_rows[:, None] >= elem_cols[None, :]
    row_tile_of = jnp.repeat(tile_rows, width)[:, None]
    ratio = pcol_count // prow_count
    home = pcol_index % prow_count

    def select_columns(block):
        shaped = block.reshape(col_tiles, ratio, width, width)
        picked = lax.dynamic_index_in_dim(shaped, pcol_index // prow_count, 1, keepdims=False)
        return picked.reshape(col_tiles * width, width)

    for step in range(BLOCKS):
        owner_row = step % prow_count
        owner_col = step % pcol_count
        first = step // pcol_count * width
        diag_start = step // prow_count * width
        panel = local[:, first : first + width]
        factor_panel = factor_local[:, first : first + width]
        diag_block, diag_factor = (
            spread(panel[diag_start : diag_start + width], "prow", owner_row),
            spread(factor_panel[diag_start : diag_start + width], "prow", owner_row),
        )
        inverse, core = diagonal_core(diag_block, diag_factor, width)
        below = row_tile_of > step
        factor_rows = jnp.where(below, factor_panel, 0.0)
        shared = product(factor_rows, core)
        halfway = jnp.where(below, product_trans(panel, inverse), 0.0) - 0.5 * shared
        finished = halfway - 0.5 * shared
        got_half, got_factor = (
            spread(halfway, "pcol", owner_col),
            spread(factor_rows, "pcol", owner_col),
        )
        keeper = prow_index == home
        col_half, col_factor = lax.psum(
            (
                jnp.where(keeper, select_columns(got_half), 0.0),
                jnp.where(keeper, select_columns(got_factor), 0.0),
            ),
            "prow",
        )
        update = product_trans(
            jnp.concatenate([got_half, got_factor], 1), jnp.concatenate([col_factor, col_half], 1)
        )
        local = local - jnp.where(lower_part, update, 0.0)
        current = local[:, first : first + width]
        diag_rows = jnp.tile(jnp.tril(core), (row_tiles, 1))
        column = jnp.where(row_tile_of == step, diag_rows, jnp.where(below, finished, current))
        column = jnp.where(pcol_index == owner_col, column, current)
        local = local.at[:, first : first + width].set(column)
    return local.reshape(row_tiles, 1, width, col_tiles, 1, width)


def solution(mesh):
    placed = (P(None, "prow", None, None, "pcol", None), P(None, "prow", None, None, "pcol", None))
    return jax.shard_map(
        on_device,
        mesh=mesh,
        in_specs=placed,
        out_specs=P(None, "prow", None, None, "pcol", None),
        check_vma=False,
    )
```

profile of v0, /device:TPU:0, one launch (start us, length us, event | category | flops | bytes accessed | tf_op | source)
XLA Modules:
  0.0 1339.8 jit_solution(16150928784970390900)
XLA Ops:
  6.5 94.1 %reduce.10 = f32[16,256,8,256]{3,2,1,0:T(8,128)} reduce(f32[16,1,256,8,1,256]{5,4,3,2,1,0:T(1,128)} %param.8, f32[]{:T(128)} %constant.182), dimensions={1,4}, to_apply=%param.8.reduce_sub_computation | reduce | bytes 67108864 | tf_op args[0]
  100.6 29.9 %copy.42 = f32[512,8,8,256]{3,1,2,0:T(8,128)} copy(f32[512,8,8,256]{3,2,1,0:T(8,128)} %bitcast.119) | data formatting | bytes 67108864
  130.5 31.1 %copy.36 = f32[4096,2048]{0,1:T(8,128)} copy(f32[4096,2048]{1,0:T(8,128)} %bitcast.120) | data formatting | bytes 67108864 | tf_op jit(solution)/shard_map/reshape | solution.py:42
  161.6 93.3 %reduce.9 = f32[16,256,8,256]{3,2,1,0:T(8,128)} reduce(f32[16,1,256,8,1,256]{5,4,3,2,1,0:T(1,128)} %param.9, f32[]{:T(128)} %constant.182), dimensions={1,4}, to_apply=%param.9.reduce_sub_computation | reduce | bytes 67108864 | tf_op args[1]
  254.9 29.9 %copy.45 = f32[512,8,8,256]{3,1,2,0:T(8,128)} copy(f32[512,8,8,256]{3,2,1,0:T(8,128)} %bitcast.118) | data formatting | bytes 67108864
  298.4 6.9 select_select_fusion.2
  305.4 30.7 %all-reduce.23.cloned.1.call-done = (f32[256,256]{0,1:T(8,128)}, f32[256,256]{0,1:T(8,128)}) async-done(((f32[256,256]{0,1:T(8,128)}, f32[256,256]{0,1:T(8,128)}), (f32[256,256]{0,1:T(8,128)}, f32[256,256]{0,1:T(8,128)})) %all-reduce.23.cloned.1.call-update) | async-done | bytes 524304 | tf_op jit(solution)/shard_map/psum | solution.py:12
  342.5 19.7 %custom-call.8 = f32[2,128,128]{1,2,0:T(8,128)S(1)} custom-call(f32[2,128,128]{2,1,0:T(8,128)S(1)} %get-tuple-element.44), custom_call_target="InvertDiagBlocksLowerTriangular" | custom-call | tf_op jit(solution)/shard_map/triangular_solve/custom-call.1 | solution.py:27
  372.5 10.7 broadcast_select_fusion.5
  383.3 175.6 %all-reduce.15.cloned.1.call-done = (f32[4096,256]{0,1:T(8,128)}, f32[4096,256]{0,1:T(8,128)}) async-done(((f32[4096,256]{0,1:T(8,128)}, f32[4096,256]{0,1:T(8,128)}), (f32[4096,256]{0,1:T(8,128)}, f32[4096,256]{0,1:T(8,128)})) %all-reduce.15.cloned.1.call-update) | async-done | bytes 8388624 | tf_op jit(solution)/shard_map/psum | solution.py:12
  559.0 7.0 reshape.187
  566.0 8.3 fusion.22
  576.5 6.7 reshape.186
  583.2 8.3 fusion.21
  600.9 96.8 %all-reduce.21.cloned.1.call-done = (f32[2048,256]{0,1:T(8,128)}, f32[2048,256]{0,1:T(8,128)}) async-done(((f32[2048,256]{0,1:T(8,128)}, f32[2048,256]{0,1:T(8,128)}), (f32[2048,256]{0,1:T(8,128)}, f32[2048,256]{0,1:T(8,128)})) %all-reduce.21.cloned.1.call-update) | async-done | bytes 4194320 | tf_op jit(solution)/shard_map/psum | solution.py:81
  697.7 65.8 %fusion = f32[4096,2048]{0,1:T(8,128)} fusion(f32[4096,2048]{0,1:T(8,128)} %copy.36, s32[4096]{0:T(1024)S(1)} %bitcast.140, s32[2048]{0:T(1024)S(1)} %bitcast.138, f32[4096,256]{0,1:T(8,128)} %get-tuple-element.80, f32[4096,256]{0,1:T(8,128)} %get-tuple-element.81, f32[2048,256]{0,1:T(8,128)} %get-tuple-element.86, f32[2048,256]{0,1:T(8,128)} %get-tuple-element.87), kind=kOutput, calls=%fused_computation.8 | convolution fusion | flops 51567919104 | bytes 79716352 | tf_op jit(solution)/shard_map/dot_general | solution.py:20
  763.6 12.5 constant_dynamic-update-slice_fusion
  777.9 45.5 %all-reduce.19.cloned.1.call-done = (f32[256,256]{0,1:T(8,128)}, f32[256,256]{0,1:T(8,128)}) async-done(((f32[256,256]{0,1:T(8,128)}, f32[256,256]{0,1:T(8,128)}), (f32[256,256]{0,1:T(8,128)}, f32[256,256]{0,1:T(8,128)})) %all-reduce.19.cloned.1.call-update) | async-done | bytes 524304 | tf_op jit(solution)/shard_map/psum | solution.py:12
  832.7 19.7 %custom-call.9 = f32[2,128,128]{1,2,0:T(8,128)S(1)} custom-call(f32[2,128,128]{2,1,0:T(8,128)S(1)} %get-tuple-element.45), custom_call_target="InvertDiagBlocksLowerTriangular" | custom-call | tf_op jit(solution)/shard_map/triangular_solve/custom-call.1 | solution.py:27
  854.5 6.0 convolution_multiply_fusion
  860.5 6.5 broadcast_select_fusion.4
  867.1 175.7 %all-reduce.13.cloned.1.call-done = (f32[4096,256]{0,1:T(8,128)}, f32[4096,256]{0,1:T(8,128)}) async-done(((f32[4096,256]{0,1:T(8,128)}, f32[4096,256]{0,1:T(8,128)}), (f32[4096,256]{0,1:T(8,128)}, f32[4096,256]{0,1:T(8,128)})) %all-reduce.13.cloned.1.call-update) | async-done | bytes 8388624 | tf_op jit(solution)/shard_map/psum | solution.py:12
  1042.7 6.7 reshape.189
  1049.5 8.3 fusion.24
  1060.0 6.8 reshape.188
  1066.8 8.3 fusion.23
  1077.8 5.9 copy.51
  1083.7 97.5 %all-reduce.17.cloned.1.call-done = (f32[2048,256]{0,1:T(8,128)}, f32[2048,256]{0,1:T(8,128)}) async-done(((f32[2048,256]{0,1:T(8,128)}, f32[2048,256]{0,1:T(8,128)}), (f32[2048,256]{0,1:T(8,128)}, f32[2048,256]{0,1:T(8,128)})) %all-reduce.17.cloned.1.call-update) | async-done | bytes 4194320 | tf_op jit(solution)/shard_map/psum | solution.py:81
  1181.2 66.0 %fusion.1 = f32[4096,2048]{0,1:T(8,128)} fusion(f32[4096,2048]{0,1:T(8,128)} %get-tuple-element.90, s32[4096]{0:T(1024)S(1)} %bitcast.141, s32[2048]{0:T(1024)S(1)} %bitcast.139, f32[4096,256]{0,1:T(8,128)} %get-tuple-element.78, f32[4096,256]{0,1:T(8,128)} %get-tuple-element.79, f32[2048,256]{0,1:T(8,128)} %get-tuple-element.82, ...), kind=kOutput, calls=%fused_computation.9 | convolution fusion | flops 51567919104 | bytes 79716352 | tf_op jit(solution)/shard_map/dot_general | solution.py:20
  1247.3 6.6 fusion.11
  1253.9 30.1 %copy.52 = f32[256,8,16,256]{3,2,1,0:T(8,128)} copy(f32[256,8,16,256]{3,1,2,0:T(8,128)} %bitcast.117) | data formatting | bytes 67108864
  1284.0 48.7 %copy.30 = f32[16,1,256,8,1,256]{5,4,3,2,1,0:T(1,128)} copy(f32[16,1,256,8,1,256]{2,0,5,3,4,1:T(8,128)} %bitcast.121) | data formatting | bytes 67108864 | tf_op jit(solution)/shard_map/reshape | solution.py:97
  (108 shorter events, 68.2 us)
Async XLA Ops:
  6.5 329.5 %all-reduce.23.cloned.1.call-start = ((), (), s32[]{:S(2)}) async-start(), calls=%async_computation.5 | async-start | bytes 1048576 | tf_op jit(solution)/shard_map/psum | solution.py:12
  287.8 271.2 %all-reduce.15.cloned.1.call-start = ((), (), s32[]{:S(2)}) async-start(), calls=%async_computation.1 | async-start | bytes 16777216 | tf_op jit(solution)/shard_map/psum | solution.py:12
  336.0 27.2 %copy-start.6 = (f32[256,256]{0,1:T(8,128)S(1)}, f32[256,256]{0,1:T(8,128)}, u32[]{:S(2)}) copy-start(f32[256,256]{0,1:T(8,128)} %get-tuple-element.88) | copy-start | bytes 786436
  372.5 10.8 copy-start.2
  383.3 314.5 %all-reduce.21.cloned.1.call-start = ((), (), s32[]{:S(2)}) async-start(), calls=%async_computation.4 | async-start | bytes 8388608 | tf_op jit(solution)/shard_map/psum | solution.py:81
  593.8 229.6 %all-reduce.19.cloned.1.call-start = ((), (), s32[]{:S(2)}) async-start(), calls=%async_computation.3 | async-start | bytes 1048576 | tf_op jit(solution)/shard_map/psum | solution.py:12
  777.8 264.9 %all-reduce.13.cloned.1.call-start = ((), (), s32[]{:S(2)}) async-start(), calls=%async_computation | async-start | bytes 16777216 | tf_op jit(solution)/shard_map/psum | solution.py:12
  823.4 30.1 %copy-start.7 = (f32[256,256]{0,1:T(8,128)S(1)}, f32[256,256]{0,1:T(8,128)}, u32[]{:S(2)}) copy-start(f32[256,256]{0,1:T(8,128)} %get-tuple-element.84) | copy-start | bytes 786436
  854.4 6.1 copy-start.3
  860.5 6.5 copy-start
  867.0 314.2 %all-reduce.17.cloned.1.call-start = ((), (), s32[]{:S(2)}) async-start(), calls=%async_computation.2 | async-start | bytes 8388608 | tf_op jit(solution)/shard_map/psum | solution.py:81
  1181.2 66.0 %copy-start.1 = (f32[4096,256]{0,1:T(8,128)S(1)}, f32[4096,256]{0,1:T(8,128)}, u32[]{:S(2)}) copy-start(f32[4096,256]{0,1:T(8,128)} %copy-done) | copy-start | bytes 12582916
  1181.2 66.0 %copy-start.4 = (f32[32,8,16,256]{3,1,2,0:T(8,128)S(1)}, f32[32,8,16,256]{3,1,2,0:T(8,128)}, u32[]{:S(2)}) copy-start(f32[32,8,16,256]{3,1,2,0:T(8,128)} %copy.51) | copy-start | bytes 12582916
  1181.2 66.0 %copy-start.5 = (f32[4096,256]{0,1:T(8,128)S(1)}, f32[4096,256]{0,1:T(8,128)}, u32[]{:S(2)}) copy-start(f32[4096,256]{0,1:T(8,128)} %get-tuple-element.103) | copy-start | bytes 12582916
Sparse Core Ops, SparseCore 0:
  287.9 48.1 all-reduce.22
  383.4 175.5 all-reduce.14
  593.9 103.7 all-reduce.20
  777.9 45.4 all-reduce.18
  867.1 175.5 all-reduce.12
  1077.4 103.7 all-reduce.16
where the time goes:
time: 1350 us; the launch traced here: 1340 us
  waiting for transfers between devices  622 us (46%)
  other arithmetic  292 us (22%)
  local copies, waits for them, and re-layouts  246 us (18%)
  matrix products  165 us (12%)
  between operations  14.1 us (1%)
    psum x4, waiting for transfers between devices, spread(): return lax.psum(block, axis)  428 us
    psum x2, waiting for transfers between devices, on_device(): lax.psum((jnp.where(keeper, select_columns(got_half), 0.0), jnp.where(kee...  194 us
    unnamed x4, other arithmetic  187 us
    dot_general x6, matrix products, product_trans(): lax.dot_general(left, right, (((1,), (1,)), ((), ())), precision=highest,...  150 us
    unnamed x29, local copies, waits for them, and re-layouts  117 us
    reshape x1, local copies, waits for them, and re-layouts, on_device(): return local.reshape(row_tiles, 1, width, col_tiles, 1, width)  48.7 us
    another operation x5, other arithmetic, diagonal_core(): lax.linalg.triangular_solve(diag_factor, identity, left_side=True, lower=...  41.3 us
    reshape x1, local copies, waits for them, and re-layouts, on_device(): local = matrix.reshape(height, col_tiles * width)  31.1 us
  transfers between devices with their start and end apart: 6, of which 6 were waited for; matrix products, arithmetic and copies ran while one was open for 2% of the time, Pallas kernels for 0%

commit v1 on v0

--- a/solution.py
+++ b/solution.py
@@ -9,7 +9,7 @@
 
 def spread(block, axis, source):
     block = jnp.where(lax.axis_index(axis) == source, block, jnp.zeros_like(block))
-    return lax.psum(block, axis)
+    return lax.all_gather(block, axis).sum(axis=0)
 
 
 def product(left, right):

time: 1350 us -> 1950 us (1.44)
  waiting for transfers between devices: 622 us -> 1240 us
  other arithmetic: 292 us -> 353 us
  local copies, waits for them, and re-layouts: 246 us -> 185 us
    all_gather x0 -> x8, waiting for transfers between devices: none -> 1030 us  [spread(): return lax.all_gather(block, axis).sum(axis=0)]
    psum x4 -> x0, waiting for transfers between devices: 428 us -> none  [spread(): return lax.psum(block, axis)]
    reduce_sum x0 -> x8, other arithmetic: none -> 68.2 us  [spread(): return lax.all_gather(block, axis).sum(axis=0)]
    reshape x1 -> x0, local copies, waits for them, and re-layouts: 31.1 us -> none  [on_device(): local = matrix.reshape(height, col_tiles * width)]
    unnamed x29 -> x34, local copies, waits for them, and re-layouts: 117 us -> 96.1 us
  transfers between devices with their start and end apart: 6 -> 10, of which waited for: 6 -> 8; matrix products, arithmetic and copies ran while one was open for 2% -> 19% of each run, Pallas kernels for 0% -> 0%
where the time goes in v1:
time: 1950 us
  waiting for transfers between devices  1240 us (64%)
  other arithmetic  353 us (18%)
  local copies, waits for them, and re-layouts  185 us (9%)
  matrix products  156 us (8%)
    all_gather x8, waiting for transfers between devices, spread(): return lax.all_gather(block, axis).sum(axis=0)  1030 us
    psum x2, waiting for transfers between devices, on_device(): lax.psum((jnp.where(keeper, select_columns(got_half), 0.0), jnp.where(kee...  202 us
    unnamed x4, other arithmetic  188 us
    dot_general x6, matrix products, product_trans(): lax.dot_general(left, right, (((1,), (1,)), ((), ())), precision=highest,...  141 us
    unnamed x34, local copies, waits for them, and re-layouts  96.1 us
    reduce_sum x8, other arithmetic, spread(): return lax.all_gather(block, axis).sum(axis=0)  68.2 us
    reshape x1, local copies, waits for them, and re-layouts, on_device(): return local.reshape(row_tiles, 1, width, col_tiles, 1, width)  48.3 us
    another operation x5, other arithmetic, diagonal_core(): lax.linalg.triangular_solve(diag_factor, identity, left_side=True, lower=...  39.4 us
  transfers between devices with their start and end apart: 10, of which 8 were waited for; matrix products, arithmetic and copies ran while one was open for 19% of the time, Pallas kernels for 0%

profile of v1, /device:TPU:0, one launch (start us, length us, event | category | flops | bytes accessed | tf_op | source)
XLA Modules:
  0.0 1946.5 jit_solution(5426693124989677940)
XLA Ops:
  6.5 93.9 %reduce.10 = f32[16,256,8,256]{3,2,1,0:T(8,128)} reduce(f32[16,1,256,8,1,256]{5,4,3,2,1,0:T(1,128)} %param.8, f32[]{:T(128)} %constant.182), dimensions={1,4}, to_apply=%param.8.reduce_sub_computation | reduce | bytes 67108864 | tf_op args[0]
  100.4 29.9 %copy.72 = f32[512,8,8,256]{3,1,2,0:T(8,128)} copy(f32[512,8,8,256]{3,2,1,0:T(8,128)} %bitcast.122) | data formatting | bytes 67108864
  132.7 93.9 %reduce.9 = f32[16,256,8,256]{3,2,1,0:T(8,128)} reduce(f32[16,1,256,8,1,256]{5,4,3,2,1,0:T(1,128)} %param.9, f32[]{:T(128)} %constant.182), dimensions={1,4}, to_apply=%param.9.reduce_sub_computation | reduce | bytes 67108864 | tf_op args[1]
  226.6 19.9 %copy.75 = f32[512,8,8,256]{3,1,2,0:T(8,128)S(1)} copy(f32[512,8,8,256]{3,2,1,0:T(8,128)} %bitcast.121) | data formatting | bytes 67108864
  246.5 11.7 copy-done
  259.3 7.5 fusion.20
  268.7 19.8 %all-gather.17.cloned.1.call-done = f32[1024,256]{1,0:T(8,128)} async-done(((f32[256,256]{1,0:T(8,128)}), f32[1024,256]{1,0:T(8,128)}) %all-gather.17.cloned.1.call-update) | async-done | bytes 1048592 | tf_op jit(solution)/shard_map/all_gather | solution.py:12
  294.3 19.7 %custom-call.8 = f32[2,128,128]{1,2,0:T(8,128)S(1)} custom-call(f32[2,128,128]{2,1,0:T(8,128)S(1)} %get-tuple-element.44), custom_call_target="InvertDiagBlocksLowerTriangular" | custom-call | tf_op jit(solution)/shard_map/triangular_solve/custom-call.1 | solution.py:27
  324.6 9.1 broadcast_select_fusion.5
  334.1 245.0 %all-gather.23.cloned.1.call-done = f32[32768,256]{1,0:T(8,128)} async-done(((f32[4096,256]{1,0:T(8,128)}), f32[32768,256]{1,0:T(8,128)}) %all-gather.23.cloned.1.call-update) | async-done | bytes 33554448 | tf_op jit(solution)/shard_map/all_gather | solution.py:12
  579.1 16.9 reduce_sum.75
  601.8 6.7 reshape.186
  608.5 8.3 fusion.21
  619.0 248.1 %all-gather.21.cloned.1.call-done = f32[32768,256]{1,0:T(8,128)} async-done(((f32[4096,256]{1,0:T(8,128)}), f32[32768,256]{1,0:T(8,128)}) %all-gather.21.cloned.1.call-update) | async-done | bytes 33554448 | tf_op jit(solution)/shard_map/all_gather | solution.py:12
  867.1 14.4 reduce_sum.74
  887.1 6.8 reshape.187
  894.0 8.3 fusion.22
  906.6 99.9 %all-reduce.7.cloned.1.call-done = (f32[2048,256]{0,1:T(8,128)}, f32[2048,256]{0,1:T(8,128)}) async-done(((f32[2048,256]{0,1:T(8,128)}, f32[2048,256]{0,1:T(8,128)}), (f32[2048,256]{0,1:T(8,128)}, f32[2048,256]{0,1:T(8,128)})) %all-reduce.7.cloned.1.call-update) | async-done | bytes 4194320 | tf_op jit(solution)/shard_map/psum | solution.py:81
  1006.4 62.0 %fusion = f32[4096,2048]{1,0:T(8,128)} fusion(f32[4096,2048]{1,0:T(8,128)} %bitcast.120, s32[2048]{0:T(1024)S(1)} %bitcast.145, s32[4096]{0:T(1024)S(1)} %bitcast.147, f32[4096,256]{0,1:T(8,128)} %copy.68, f32[4096,256]{0,1:T(8,128)} %copy.67, f32[2048,256]{0,1:T(8,128)} %get-tuple-element.80, f32[2048,256]{0,1:T(8,128)} %get-tuple-element.81), kind=kOutput, calls=%fused_computation.8 | convolution fusion | flops 51567919104 | bytes 79716352 | tf_op jit(solution)/shard_map/dot_general | solution.py:20
  1083.7 19.7 %custom-call.9 = f32[2,128,128]{1,2,0:T(8,128)S(1)} custom-call(f32[2,128,128]{2,1,0:T(8,128)S(1)} %get-tuple-element.45), custom_call_target="InvertDiagBlocksLowerTriangular" | custom-call | tf_op jit(solution)/shard_map/triangular_solve/custom-call.1 | solution.py:27
  1115.9 6.6 broadcast_select_fusion.4
  1122.8 271.9 %all-gather.31.cloned.1.call-done = f32[32768,256]{1,0:T(8,128)} async-done(((f32[4096,256]{1,0:T(8,128)}), f32[32768,256]{1,0:T(8,128)}) %all-gather.31.cloned.1.call-update) | async-done | bytes 33554448 | tf_op jit(solution)/shard_map/all_gather | solution.py:12
  1394.7 17.3 reduce_sum.79
  1417.9 6.6 reshape.188
  1424.5 8.3 fusion.23
  1435.1 248.1 %all-gather.29.cloned.1.call-done = f32[32768,256]{1,0:T(8,128)} async-done(((f32[4096,256]{1,0:T(8,128)}), f32[32768,256]{1,0:T(8,128)}) %all-gather.29.cloned.1.call-update) | async-done | bytes 33554448 | tf_op jit(solution)/shard_map/all_gather | solution.py:12
  1683.2 14.3 reduce_sum.78
  1703.2 6.8 reshape.189
  1710.0 8.3 fusion.24
  1720.6 101.8 %all-reduce.5.cloned.1.call-done = (f32[2048,256]{0,1:T(8,128)}, f32[2048,256]{0,1:T(8,128)}) async-done(((f32[2048,256]{0,1:T(8,128)}, f32[2048,256]{0,1:T(8,128)}), (f32[2048,256]{0,1:T(8,128)}, f32[2048,256]{0,1:T(8,128)})) %all-reduce.5.cloned.1.call-update) | async-done | bytes 4194320 | tf_op jit(solution)/shard_map/psum | solution.py:81
  1822.5 62.3 %fusion.1 = f32[4096,2048]{1,0:T(8,128)} fusion(f32[4096,2048]{1,0:T(8,128)} %get-tuple-element.92, s32[2048]{0:T(1024)S(1)} %bitcast.146, s32[4096]{0:T(1024)S(1)} %bitcast.148, f32[4096,256]{0,1:T(8,128)} %copy.71, f32[4096,256]{0,1:T(8,128)} %copy.70, f32[2048,256]{0,1:T(8,128)} %get-tuple-element.78, f32[2048,256]{0,1:T(8,128)} %get-tuple-element.79), kind=kOutput, calls=%fused_computation.9 | convolution fusion | flops 51567919104 | bytes 79716352 | tf_op jit(solution)/shard_map/dot_general | solution.py:20
  1890.8 48.3 %reshape.239 = f32[16,1,256,8,1,256]{5,4,3,2,1,0:T(1,128)} reshape(f32[4096,2048]{1,0:T(8,128)} %fusion.11) | data formatting | bytes 67108864 | tf_op jit(solution)/shard_map/reshape | solution.py:97
  (127 shorter events, 98.0 us)
Async XLA Ops:
  6.5 260.6 %all-gather.19.cloned.1.call-start = ((), (), s32[]{:S(2)}) async-start(), calls=%async_computation.1 | async-start | bytes 1310720 | tf_op jit(solution)/shard_map/all_gather | solution.py:12
  132.1 156.3 %all-gather.17.cloned.1.call-start = ((), (), s32[]{:S(2)}) async-start(), calls=%async_computation | async-start | bytes 1310720 | tf_op jit(solution)/shard_map/all_gather | solution.py:12
  246.5 11.7 copy-start
  259.1 320.0 %all-gather.23.cloned.1.call-start = ((), (), s32[]{:S(2)}) async-start(), calls=%async_computation.3 | async-start | bytes 37748736 | tf_op jit(solution)/shard_map/all_gather | solution.py:12
  266.9 600.2 %all-gather.21.cloned.1.call-start = ((), (), s32[]{:S(2)}) async-start(), calls=%async_computation.2 | async-start | bytes 37748736 | tf_op jit(solution)/shard_map/all_gather | solution.py:12
  324.6 9.2 copy-start.1
  333.8 672.6 %all-reduce.7.cloned.1.call-start = ((), (), s32[]{:S(2)}) async-start(), calls=%async_computation.9 | async-start | bytes 8388608 | tf_op jit(solution)/shard_map/psum | solution.py:81
  904.5 173.5 %all-gather.25.cloned.1.call-start = ((), (), s32[]{:S(2)}) async-start(), calls=%async_computation.4 | async-start | bytes 1310720 | tf_op jit(solution)/shard_map/all_gather | solution.py:12
  905.0 199.5 %all-gather.27.cloned.1.call-start = ((), (), s32[]{:S(2)}) async-start(), calls=%async_computation.5 | async-start | bytes 1310720 | tf_op jit(solution)/shard_map/all_gather | solution.py:12
  1006.4 62.0 %copy-start.2 = (f32[4096,256]{1,0:T(8,128)S(1)}, f32[4096,256]{1,0:T(8,128)}, u32[]{:S(2)}) copy-start(f32[4096,256]{1,0:T(8,128)} %copy-done.1) | copy-start | bytes 12582916
  1006.4 62.0 %copy-start.7 = (f32[4096,256]{1,0:T(8,128)S(1)}, f32[4096,256]{1,0:T(8,128)}, u32[]{:S(2)}) copy-start(f32[4096,256]{1,0:T(8,128)} %get-tuple-element.91) | copy-start | bytes 12582916
  1074.4 2.0 copy-start.5
  1077.2 317.6 %all-gather.31.cloned.1.call-start = ((), (), s32[]{:S(2)}) async-start(), calls=%async_computation.7 | async-start | bytes 37748736 | tf_op jit(solution)/shard_map/all_gather | solution.py:12
  1077.9 605.3 %all-gather.29.cloned.1.call-start = ((), (), s32[]{:S(2)}) async-start(), calls=%async_computation.6 | async-start | bytes 37748736 | tf_op jit(solution)/shard_map/all_gather | solution.py:12
  1109.4 6.5 copy-start.6
  1115.9 6.9 copy-start.3
  1122.8 699.7 %all-reduce.5.cloned.1.call-start = ((), (), s32[]{:S(2)}) async-start(), calls=%async_computation.8 | async-start | bytes 8388608 | tf_op jit(solution)/shard_map/psum | solution.py:81
  1822.5 62.3 %copy-start.4 = (f32[4096,256]{1,0:T(8,128)S(1)}, f32[4096,256]{1,0:T(8,128)}, u32[]{:S(2)}) copy-start(f32[4096,256]{1,0:T(8,128)} %copy-done.3) | copy-start | bytes 12582916
  1822.5 62.3 %copy-start.8 = (f32[4096,256]{1,0:T(8,128)S(1)}, f32[4096,256]{1,0:T(8,128)}, u32[]{:S(2)}) copy-start(f32[4096,256]{1,0:T(8,128)} %get-tuple-element.95) | copy-start | bytes 12582916
Sparse Core Ops, SparseCore 0:
  132.2 29.2 all-gather.18
  259.2 29.2 all-gather.16
  290.0 289.0 all-gather.22
  580.5 286.5 all-gather.20
  904.6 101.8 all-reduce.6
  1008.1 26.4 all-gather.24
  1077.3 27.1 all-gather.26
  1106.1 288.5 all-gather.30
  1396.4 286.7 all-gather.28
  1720.6 101.8 all-reduce.4
